TPU v7x, 32 devices: a whole 2x2x4 slice. The times are simulated.
32 devices in a mesh: dp: 8 (over z, x), mp: 4 (over y, core).
Axes of the slice: x: 2, y: 2, z: 4, core: 2. Of those that a mesh axis runs over, the one named last changes fastest.
Arguments:
- tokens: bfloat16 [16384, 1024], P(('dp', 'mp')), may hold values from -6 to 6
- segments: int32 [8, 2048], P('dp'), may hold values from 0 to 7, never falling along the last dimension, each value on 1 to 512 neighbouring positions
- attn_norm_gain: float32 [1024], replicated, may hold values from 0.1 to 1.9
- attn_norm_bias: float32 [1024], replicated, may hold values from -3 to 3
- query_weight: bfloat16 [1024, 1024], P(None, 'mp'), may hold values from -0.1875 to 0.1875
- key_weight: bfloat16 [1024, 1024], P(None, 'mp'), may hold values from -0.1875 to 0.1875
- value_weight: bfloat16 [1024, 1024], P(None, 'mp'), may hold values from -0.1875 to 0.1875
- output_weight: bfloat16 [1024, 1024], P('mp'), may hold values from -1.5 to 1.5
- mlp_norm_gain: float32 [1024], replicated, may hold values from 0.1 to 1.9
- mlp_norm_bias: float32 [1024], replicated, may hold values from -3 to 3
- gate_weight: bfloat16 [1024, 4096], P(None, 'mp'), may hold values from -0.1875 to 0.1875
- up_weight: bfloat16 [1024, 4096], P(None, 'mp'), may hold values from -0.1875 to 0.1875
- down_weight: bfloat16 [4096, 1024], P('mp'), may hold values from -0.125 to 0.125
- grad_out: bfloat16 [16384, 1024], P(('dp', 'mp')), may hold values from -6 to 6
Outputs:
- block_out: bfloat16 [16384, 1024], P(('dp', 'mp'))
- grad_tokens: float32 [16384, 1024], P(('dp', 'mp'))
- grad_attn_norm_gain: float32 [1024], replicated
- grad_attn_norm_bias: float32 [1024], replicated
- grad_query_weight: float32 [1024, 1024], P(None, 'mp')
- grad_key_weight: float32 [1024, 1024], P(None, 'mp')
- grad_value_weight: float32 [1024, 1024], P(None, 'mp')
- grad_output_weight: float32 [1024, 1024], P('mp')
- grad_mlp_norm_gain: float32 [1024], replicated
- grad_mlp_norm_bias: float32 [1024], replicated
- grad_gate_weight: float32 [1024, 4096], P(None, 'mp')
- grad_up_weight: float32 [1024, 4096], P(None, 'mp')
- grad_down_weight: float32 [4096, 1024], P('mp')
Inputs may be any that keep to these rules, and one draw needn't show every extreme that they name: `segments`: within each row of 2048 tokens the window numbers start at 0, never fall, and each of the 8 numbers holds 1 to 512 tokens.
All inputs are finite; a program needn't handle non-finite values.
Results may differ from a plain program's by a relative error of at most 0.014.
The roundings to bfloat16 on the way count: a program that leaves them out, or rounds other values in their place, can miss the bound.
Values may be sent and summed in bfloat16 or wider, within the bound.
A program may use at most 192 MiB of HBM per device.

v0:
```python
import jax
import jax.numpy as jnp
from jax import lax
from jax.sharding import PartitionSpec as P

HEAD_DIM = 64
QBLK = 512


epsilon = 1e-05


def contract_rows(left, right):
    return lax.dot_general(
        left, right, (((0,), (0,)), ((), ())), preferred_element_type=jnp.float32
    )


def contract_cols(left, right):
    return lax.dot_general(
        left, right, (((1,), (1,)), ((), ())), preferred_element_type=jnp.float32
    )


def normalize(values):
    center = values - jnp.mean(values, axis=-1, keepdims=True)
    inverse = lax.rsqrt(jnp.mean(center * center, axis=-1, keepdims=True) + epsilon)
    return (center * inverse, inverse)


def norm_back(incoming, scaled, inverse, gain):
    gain_part = jnp.sum(incoming * scaled, axis=0)
    shift_part = jnp.sum(incoming, axis=0)
    along = incoming * gain
    mean_plain = jnp.mean(along, axis=-1, keepdims=True)
    mean_mixed = jnp.mean(along * scaled, axis=-1, keepdims=True)
    return (inverse * (along - mean_plain - scaled * mean_mixed), gain_part, shift_part)


def rotary_tables(segments, head_dim):
    row_count, seq_len = segments.shape
    places = jnp.arange(seq_len, dtype=jnp.int32)
    changes = jnp.concatenate(
        [
            jnp.ones((row_count, 1), jnp.int32),
            (segments[:, 1:] != segments[:, :-1]).astype(jnp.int32),
        ],
        axis=1,
    )
    starts = lax.cummax(jnp.where(changes > 0, places[None, :], 0), axis=1)
    position = (places[None, :] - starts).astype(jnp.float32).reshape(row_count * seq_len)
    half_dim = head_dim // 2
    frequency = 10000.0 ** (-2.0 * jnp.arange(half_dim, dtype=jnp.float32) / head_dim)
    angles = position[:, None] * frequency[None, :]
    cosine_table = jnp.concatenate([jnp.cos(angles), jnp.cos(angles)], axis=1)
    sine_table = jnp.concatenate([jnp.sin(angles), jnp.sin(angles)], axis=1)
    return (cosine_table, sine_table)


def turn_half(values):
    half_dim = values.shape[-1] // 2
    return jnp.concatenate([-values[..., half_dim:], values[..., :half_dim]], axis=-1)


def rotate(values, cosine_table, sine_table):
    return values * cosine_table[:, None, :] + turn_half(values) * sine_table[:, None, :]


def unrotate(values, cosine_table, sine_table):
    return values * cosine_table[:, None, :] - turn_half(values) * sine_table[:, None, :]


def per_device(
    tokens,
    segments,
    attn_norm_gain,
    attn_norm_bias,
    query_weight,
    key_weight,
    value_weight,
    output_weight,
    mlp_norm_gain,
    mlp_norm_bias,
    gate_weight,
    up_weight,
    down_weight,
    grad_out,
):
    row_count, seq_len = segments.shape
    row_tokens = row_count * seq_len
    local_heads = query_weight.shape[1] // HEAD_DIM
    score_scale = HEAD_DIM ** (-0.5)
    seg_flat = segments.reshape(row_tokens)
    cosine_table, sine_table = rotary_tables(segments, HEAD_DIM)
    inputs = tokens.astype(jnp.float32)
    attn_scaled, attn_inverse = normalize(inputs)
    attn_normed = (attn_scaled * attn_norm_gain + attn_norm_bias).astype(jnp.bfloat16)
    attn_full = lax.all_gather(attn_normed, "mp", axis=0, tiled=True)
    query_rot = rotate(
        jnp.dot(attn_full, query_weight, preferred_element_type=jnp.float32).reshape(
            row_tokens, local_heads, HEAD_DIM
        ),
        cosine_table,
        sine_table,
    ).astype(jnp.bfloat16)
    key_rot = rotate(
        jnp.dot(attn_full, key_weight, preferred_element_type=jnp.float32).reshape(
            row_tokens, local_heads, HEAD_DIM
        ),
        cosine_table,
        sine_table,
    ).astype(jnp.bfloat16)
    value_low = (
        jnp.dot(attn_full, value_weight, preferred_element_type=jnp.float32)
        .astype(jnp.bfloat16)
        .reshape(row_tokens, local_heads, HEAD_DIM)
    )
    block_starts = jnp.arange(row_tokens // QBLK, dtype=jnp.int32) * QBLK

    def score_block(offset):
        row_start = offset // seq_len * seq_len
        query_block = lax.dynamic_slice_in_dim(query_rot, offset, QBLK, 0)
        query_seg = lax.dynamic_slice_in_dim(seg_flat, offset, QBLK, 0)
        raw_score = jnp.einsum(
            "qhd,khd->hqk", query_block, key_rot, preferred_element_type=jnp.float32
        )
        same_window = query_seg[:, None] == seg_flat[None, :]
        scores = jnp.where(same_window[None], raw_score * score_scale, -1e30)
        return (scores, row_start, query_block, key_rot, value_low)

    def forward_block(offset):
        scores, row_start, query_block, key_block, value_block = score_block(offset)
        row_max = jnp.max(scores, axis=-1, keepdims=True)
        log_total = row_max + jnp.log(jnp.sum(jnp.exp(scores - row_max), axis=-1, keepdims=True))
        attn_prob = jnp.exp(scores - log_total)
        block_heads = jnp.einsum(
            "hqk,khd->qhd",
            attn_prob.astype(jnp.bfloat16),
            value_block,
            preferred_element_type=jnp.float32,
        )
        return (block_heads.astype(jnp.bfloat16), log_total[..., 0])

    head_blocks, log_totals = lax.map(forward_block, block_starts)
    head_out = head_blocks.reshape(row_tokens, local_heads * HEAD_DIM)
    middle = inputs + lax.psum_scatter(
        jnp.dot(head_out, output_weight, preferred_element_type=jnp.float32),
        "mp",
        scatter_dimension=0,
        tiled=True,
    )
    mlp_scaled, mlp_inverse = normalize(middle)
    mlp_normed = (mlp_scaled * mlp_norm_gain + mlp_norm_bias).astype(jnp.bfloat16)
    mlp_full = lax.all_gather(mlp_normed, "mp", axis=0, tiled=True)
    gate_act = jnp.dot(mlp_full, gate_weight, preferred_element_type=jnp.float32)
    up_act = jnp.dot(mlp_full, up_weight, preferred_element_type=jnp.float32)
    sig_gate = jax.nn.sigmoid(gate_act)
    hidden = (gate_act * sig_gate * up_act).astype(jnp.bfloat16)
    block_out = (
        middle
        + lax.psum_scatter(
            jnp.dot(hidden, down_weight, preferred_element_type=jnp.float32).astype(jnp.bfloat16),
            "mp",
            scatter_dimension=0,
            tiled=True,
        ).astype(jnp.float32)
    ).astype(jnp.bfloat16)
    upstream = grad_out.astype(jnp.float32)
    cot_full = lax.all_gather(grad_out, "mp", axis=0, tiled=True)
    grad_down = contract_rows(hidden, cot_full)
    grad_hidden = contract_cols(cot_full, down_weight)
    grad_gate = (grad_hidden * up_act * (sig_gate + gate_act * sig_gate * (1.0 - sig_gate))).astype(
        jnp.bfloat16
    )
    grad_up = (grad_hidden * gate_act * sig_gate).astype(jnp.bfloat16)
    grad_gate_w = contract_rows(mlp_full, grad_gate)
    grad_up_w = contract_rows(mlp_full, grad_up)
    grad_mlp_normed = lax.psum_scatter(
        contract_cols(grad_gate, gate_weight) + contract_cols(grad_up, up_weight),
        "mp",
        scatter_dimension=0,
        tiled=True,
    )
    middle_part, mlp_gain_part, mlp_shift_part = norm_back(
        grad_mlp_normed, mlp_scaled, mlp_inverse, mlp_norm_gain
    )
    grad_middle = upstream + middle_part
    attn_cot = lax.all_gather(grad_middle.astype(jnp.bfloat16), "mp", axis=0, tiled=True)
    grad_output_w = contract_rows(head_out, attn_cot)
    grad_head = (
        contract_cols(attn_cot, output_weight)
        .astype(jnp.bfloat16)
        .reshape(row_tokens, local_heads, HEAD_DIM)
    )

    def backward_block(carry, element):
        key_acc, value_acc = carry
        offset, log_total = element
        scores, row_start, query_block, key_block, value_block = score_block(offset)
        attn_prob = jnp.exp(scores - log_total[..., None])
        head_block = lax.dynamic_slice_in_dim(grad_head, offset, QBLK, 0)
        grad_prob = jnp.einsum(
            "qhd,khd->hqk", head_block, value_block, preferred_element_type=jnp.float32
        )
        grad_score = attn_prob * (
            grad_prob - jnp.sum(attn_prob * grad_prob, axis=-1, keepdims=True)
        )
        grad_raw = (grad_score * score_scale).astype(jnp.bfloat16)
        query_part = jnp.einsum(
            "hqk,khd->qhd", grad_raw, key_block, preferred_element_type=jnp.float32
        )
        key_part = jnp.einsum(
            "hqk,qhd->khd", grad_raw, query_block, preferred_element_type=jnp.float32
        )
        value_part = jnp.einsum(
            "hqk,qhd->khd",
            attn_prob.astype(jnp.bfloat16),
            head_block,
            preferred_element_type=jnp.float32,
        )
        key_rows = key_acc
        value_rows = value_acc
        key_acc = key_rows + key_part
        value_acc = value_rows + value_part
        return ((key_acc, value_acc), query_part)

    zero_acc = jnp.zeros((row_tokens, local_heads, HEAD_DIM), jnp.float32)
    (key_acc, value_acc), query_parts = lax.scan(
        backward_block, (zero_acc, zero_acc), (block_starts, log_totals)
    )
    grad_qrot = query_parts.reshape(row_tokens, local_heads, HEAD_DIM)
    grad_query = (
        unrotate(grad_qrot, cosine_table, sine_table)
        .astype(jnp.bfloat16)
        .reshape(row_tokens, local_heads * HEAD_DIM)
    )
    grad_key = (
        unrotate(key_acc, cosine_table, sine_table)
        .astype(jnp.bfloat16)
        .reshape(row_tokens, local_heads * HEAD_DIM)
    )
    grad_value = value_acc.astype(jnp.bfloat16).reshape(row_tokens, local_heads * HEAD_DIM)
    grad_query_w = contract_rows(attn_full, grad_query)
    grad_key_w = contract_rows(attn_full, grad_key)
    grad_value_w = contract_rows(attn_full, grad_value)
    key_rows = grad_key
    value_rows = grad_value
    grad_attn_normed = lax.psum_scatter(
        contract_cols(grad_query, query_weight)
        + contract_cols(key_rows, key_weight)
        + contract_cols(value_rows, value_weight),
        "mp",
        scatter_dimension=0,
        tiled=True,
    )
    input_part, attn_gain_part, attn_shift_part = norm_back(
        grad_attn_normed, attn_scaled, attn_inverse, attn_norm_gain
    )
    grad_tokens = grad_middle + input_part
    gain_attn, shift_attn, gain_mlp, shift_mlp = lax.psum(
        (attn_gain_part, attn_shift_part, mlp_gain_part, mlp_shift_part), ("dp", "mp")
    )
    summed_query, summed_key, summed_value, summed_output, summed_gate, summed_up, summed_down = (
        lax.psum(
            (
                grad_query_w,
                grad_key_w,
                grad_value_w,
                grad_output_w,
                grad_gate_w,
                grad_up_w,
                grad_down,
            ),
            "dp",
        )
    )
    return (
        block_out,
        grad_tokens,
        gain_attn,
        shift_attn,
        summed_query,
        summed_key,
        summed_value,
        summed_output,
        gain_mlp,
        shift_mlp,
        summed_gate,
        summed_up,
        summed_down,
    )


def solution(mesh):
    in_specs = (
        P(("dp", "mp"), None),
        P("dp", None),
        P(),
        P(),
        P(None, "mp"),
        P(None, "mp"),
        P(None, "mp"),
        P("mp", None),
        P(),
        P(),
        P(None, "mp"),
        P(None, "mp"),
        P("mp", None),
        P(("dp", "mp"), None),
    )
    out_specs = (
        P(("dp", "mp"), None),
        P(("dp", "mp"), None),
        P(),
        P(),
        P(None, "mp"),
        P(None, "mp"),
        P(None, "mp"),
        P("mp", None),
        P(),
        P(),
        P(None, "mp"),
        P(None, "mp"),
        P("mp", None),
    )
    return jax.shard_map(
        per_device, mesh=mesh, in_specs=in_specs, out_specs=out_specs, check_vma=False
    )
```

profile of v0, /device:TPU:0, one launch (start us, length us, event | category | flops | bytes accessed | tf_op | source)
XLA Modules:
  0.0 1462.9 jit_solution(2266541949724565049)
XLA Ops:
  17.0 34.2 %all-gather.5.cloned.1.call-done = bf16[2048,1024]{1,0:T(8,128)(2,1)} async-done(((bf16[512,1024]{1,0:T(8,128)(2,1)}), bf16[2048,1024]{1,0:T(8,128)(2,1)}) %all-gather.5.cloned.1.call-update) | async-done | bytes 4194320 | tf_op jit(solution)/shard_map/all_gather | solution.py:98
  61.7 71.3 %while.27 = (s32[]{:T(128)}, bf16[4,512,4,64]{1,3,2,0:T(8,128)(2,1)}, f32[4,4,512]{2,1,0:T(4,128)S(1)}, s32[4]{0:T(128)S(1)}, s32[2048]{0:T(1024)S(1)}, /*index=...) while((s32[]{:T(128)}, ...), condition=%wide.region_7.8_spmd, body=%wide.region_4.7_spmd.sunk | while | flops 1121056768 | bytes 61421784 | solution.py:144
  140.9 71.5 %reduce-scatter.5.cloned.1.call-done = f32[512,1024]{1,0:T(8,128)} async-done(((f32[2048,1024]{1,0:T(8,128)}), f32[512,1024]{1,0:T(8,128)}) %reduce-scatter.5.cloned.1.call-update) | async-done | bytes 2097168 | tf_op jit(solution)/shard_map/reduce_scatter | solution.py:146
  217.9 34.0 %all-gather.7.cloned.1.call-done = bf16[2048,1024]{1,0:T(8,128)(2,1)} async-done(((bf16[512,1024]{1,0:T(8,128)(2,1)}), bf16[2048,1024]{1,0:T(8,128)(2,1)}) %all-gather.7.cloned.1.call-update) | async-done | bytes 4194320 | tf_op jit(solution)/shard_map/all_gather | solution.py:154
  251.9 11.4 fusion.108
  270.4 17.4 %all-gather.9.cloned.1.call-done = bf16[2048,1024]{1,0:T(8,128)(2,1)} async-done(((bf16[512,1024]{1,0:T(8,128)(2,1)}), bf16[2048,1024]{1,0:T(8,128)(2,1)}) %all-gather.9.cloned.1.call-update) | async-done | bytes 4194320 | tf_op jit(solution)/shard_map/all_gather | solution.py:169
  287.8 15.7 %multiply_convert_fusion.1 = (bf16[2048,1024]{1,0:T(8,128)(2,1)}, bf16[2048,1024]{1,0:T(8,128)(2,1)}, bf16[2048,1024]{1,0:T(8,128)(2,1)}) fusion(f32[2048,1024]{1,0:T(8,128)} %fusion.107, f32[2048,1024]{1,0:T(8,128)} %fusion.108, bf16[2048,1024]{1,0:T(8,128)(2,1)} %all-gather.9.cloned.1.call-done, bf16[1024,1024]{1,0:T(8,128)(2,1)S(1)} %copy-done), kind=kOutput, calls=%fused_computation.61 | convolution fusion | flops 4326424576 | bytes 35651584 | tf_op jit(solution)/shard_map/dot_general | solution.py:20
  326.2 63.0 %reduce-scatter.9.cloned.1.call-done = f32[512,1024]{1,0:T(8,128)} async-done(((f32[2048,1024]{1,0:T(8,128)}), f32[512,1024]{1,0:T(8,128)}) %reduce-scatter.9.cloned.1.call-update) | async-done | bytes 2097168 | tf_op jit(solution)/shard_map/reduce_scatter | solution.py:178
  392.2 43.9 %reduce-scatter.7.cloned.1.call-done = bf16[512,1024]{1,0:T(8,128)(2,1)} async-done(((bf16[2048,1024]{1,0:T(8,128)(2,1)}), bf16[512,1024]{1,0:T(8,128)(2,1)}) %reduce-scatter.7.cloned.1.call-update) | async-done | bytes 1048592 | tf_op jit(solution)/shard_map/reduce_scatter | solution.py:161
  441.4 34.5 %all-gather.11.cloned.1.call-done = bf16[2048,1024]{1,0:T(8,128)(2,1)} async-done(((bf16[512,1024]{1,0:T(8,128)(2,1)}), bf16[2048,1024]{1,0:T(8,128)(2,1)}) %all-gather.11.cloned.1.call-update) | async-done | bytes 4194320 | tf_op jit(solution)/shard_map/all_gather | solution.py:188
  480.5 351.4 %while.28 = (s32[]{:T(128)}, f32[2048,4,64]{0,2,1:T(8,128)}, f32[2048,4,64]{0,2,1:T(8,128)}, f32[4,512,4,64]{1,0,3,2:T(4,128)}, s32[4]{0:T(128)S(1)}, /*index=5*...) while((s32[]{:T(128)}, f32[2048,4,64]{0,2,1:T(8,128)}, ...), condition=%wide.region_17.18_spmd.clone, body=%wide.region_15.17_spmd.clone.sunk | while | flops 2796560384 | bytes 247003472 | solution.py:228
  504.1 24.4 %fusion.203 = f32[1,512,4,64]{1,3,2,0:T(8,128)} fusion(bf16[2048,4,64]{0,2,1:T(8,128)(2,1)} %copy-done.3, f32[4,512,2048]{2,1,0:T(8,128)} %fusion.199, f32[4,512,2048]{2,1,0:T(8,128)} %copy-done.2, f32[4,512]{1,0:T(4,128)S(1)} %dynamic-slice_bitcast_fusion.2, pred[512,2048]{1,0:T(8,128)(4,1)S(1)} %broadcast_compare_fusion.5), kind=kOutput, calls=%fused_computation.40.clone.1 | convolution fusion | flops 583012352 | bytes 36184064 | tf_op jit(solution)/shard_map/while/body/eval_jaxpr/hqk,khd->qhd/dot_general | solution.py:209
  528.5 25.8 %fusion.201 = f32[2048,4,64]{0,2,1:T(8,128)} fusion(f32[4,512,2048]{2,1,0:T(8,128)} %fusion.199, f32[4,512,2048]{2,1,0:T(8,128)} %copy-done.2, f32[4,512]{1,0:T(4,128)S(1)} %dynamic-slice_bitcast_fusion.2, pred[512,2048]{1,0:T(8,128)(4,1)S(1)} %broadcast_compare_fusion.5, f32[2048,4,64]{0,2,1:T(8,128)} %get-tuple-element.448, pred[]{:T(512)S(6)} %compare.3, ...), kind=kOutput, calls=%fused_computation.38.clone.1 | convolution fusion | flops 584060928 | bytes 73678856 | tf_op jit(solution)/shard_map/while/body/eval_jaxpr/hqk,qhd->khd/dot_general | solution.py:212
  555.9 11.1 dynamic_update_slice.20
  591.8 24.4 %fusion.203 = f32[1,512,4,64]{1,3,2,0:T(8,128)} fusion(bf16[2048,4,64]{0,2,1:T(8,128)(2,1)} %copy-done.3, f32[4,512,2048]{2,1,0:T(8,128)} %fusion.199, f32[4,512,2048]{2,1,0:T(8,128)} %copy-done.2, f32[4,512]{1,0:T(4,128)S(1)} %dynamic-slice_bitcast_fusion.2, pred[512,2048]{1,0:T(8,128)(4,1)S(1)} %broadcast_compare_fusion.5), kind=kOutput, calls=%fused_computation.40.clone.1 | convolution fusion | flops 583012352 | bytes 36184064 | tf_op jit(solution)/shard_map/while/body/eval_jaxpr/hqk,khd->qhd/dot_general | solution.py:209
  616.2 26.4 %fusion.201 = f32[2048,4,64]{0,2,1:T(8,128)} fusion(f32[4,512,2048]{2,1,0:T(8,128)} %fusion.199, f32[4,512,2048]{2,1,0:T(8,128)} %copy-done.2, f32[4,512]{1,0:T(4,128)S(1)} %dynamic-slice_bitcast_fusion.2, pred[512,2048]{1,0:T(8,128)(4,1)S(1)} %broadcast_compare_fusion.5, f32[2048,4,64]{0,2,1:T(8,128)} %get-tuple-element.448, pred[]{:T(512)S(6)} %compare.3, ...), kind=kOutput, calls=%fused_computation.38.clone.1 | convolution fusion | flops 584060928 | bytes 73678856 | tf_op jit(solution)/shard_map/while/body/eval_jaxpr/hqk,qhd->khd/dot_general | solution.py:212
  680.0 24.4 %fusion.203 = f32[1,512,4,64]{1,3,2,0:T(8,128)} fusion(bf16[2048,4,64]{0,2,1:T(8,128)(2,1)} %copy-done.3, f32[4,512,2048]{2,1,0:T(8,128)} %fusion.199, f32[4,512,2048]{2,1,0:T(8,128)} %copy-done.2, f32[4,512]{1,0:T(4,128)S(1)} %dynamic-slice_bitcast_fusion.2, pred[512,2048]{1,0:T(8,128)(4,1)S(1)} %broadcast_compare_fusion.5), kind=kOutput, calls=%fused_computation.40.clone.1 | convolution fusion | flops 583012352 | bytes 36184064 | tf_op jit(solution)/shard_map/while/body/eval_jaxpr/hqk,khd->qhd/dot_general | solution.py:209
  704.4 26.4 %fusion.201 = f32[2048,4,64]{0,2,1:T(8,128)} fusion(f32[4,512,2048]{2,1,0:T(8,128)} %fusion.199, f32[4,512,2048]{2,1,0:T(8,128)} %copy-done.2, f32[4,512]{1,0:T(4,128)S(1)} %dynamic-slice_bitcast_fusion.2, pred[512,2048]{1,0:T(8,128)(4,1)S(1)} %broadcast_compare_fusion.5, f32[2048,4,64]{0,2,1:T(8,128)} %get-tuple-element.448, pred[]{:T(512)S(6)} %compare.3, ...), kind=kOutput, calls=%fused_computation.38.clone.1 | convolution fusion | flops 584060928 | bytes 73678856 | tf_op jit(solution)/shard_map/while/body/eval_jaxpr/hqk,qhd->khd/dot_general | solution.py:212
  732.3 11.1 dynamic_update_slice.20
  768.1 24.4 %fusion.203 = f32[1,512,4,64]{1,3,2,0:T(8,128)} fusion(bf16[2048,4,64]{0,2,1:T(8,128)(2,1)} %copy-done.3, f32[4,512,2048]{2,1,0:T(8,128)} %fusion.199, f32[4,512,2048]{2,1,0:T(8,128)} %copy-done.2, f32[4,512]{1,0:T(4,128)S(1)} %dynamic-slice_bitcast_fusion.2, pred[512,2048]{1,0:T(8,128)(4,1)S(1)} %broadcast_compare_fusion.5), kind=kOutput, calls=%fused_computation.40.clone.1 | convolution fusion | flops 583012352 | bytes 36184064 | tf_op jit(solution)/shard_map/while/body/eval_jaxpr/hqk,khd->qhd/dot_general | solution.py:209
  792.5 26.3 %fusion.201 = f32[2048,4,64]{0,2,1:T(8,128)} fusion(f32[4,512,2048]{2,1,0:T(8,128)} %fusion.199, f32[4,512,2048]{2,1,0:T(8,128)} %copy-done.2, f32[4,512]{1,0:T(4,128)S(1)} %dynamic-slice_bitcast_fusion.2, pred[512,2048]{1,0:T(8,128)(4,1)S(1)} %broadcast_compare_fusion.5, f32[2048,4,64]{0,2,1:T(8,128)} %get-tuple-element.448, pred[]{:T(512)S(6)} %compare.3, ...), kind=kOutput, calls=%fused_computation.38.clone.1 | convolution fusion | flops 584060928 | bytes 73678856 | tf_op jit(solution)/shard_map/while/body/eval_jaxpr/hqk,qhd->khd/dot_general | solution.py:212
  883.8 38.3 %reduce-scatter.11.cloned.1.call-done = f32[512,1024]{1,0:T(8,128)} async-done(((f32[2048,1024]{1,0:T(8,128)}), f32[512,1024]{1,0:T(8,128)}) %reduce-scatter.11.cloned.1.call-update) | async-done | bytes 2097168 | tf_op jit(solution)/shard_map/reduce_scatter | solution.py:248
  924.6 45.0 %all-reduce = (f32[1024]{0:T(1024)}, f32[1024]{0:T(1024)}, f32[1024]{0:T(1024)}, f32[1024]{0:T(1024)}) all-reduce(f32[1024]{0:T(1024)S(1)} %get-tuple-element.171, f32[1024]{0:T(1024)S(1)} %get-tuple-element.176, f32[1024]{0:T(1024)S(1)} %copy-done.40, f32[1024]{0:T(1024)S(1)} %copy-done.41), channel_id=1, replica_groups=mesh['dp'=8,'mp'=4] {'dp','mp'}, use_global_device_ids=true, to_apply=%region_22.23 | all-reduce | flops 4096 | bytes 32768 | tf_op jit(solution)/shard_map/psum | solution.py:260
  974.0 466.1 %all-reduce.4.cloned.1.call-done = (f32[1024,256]{1,0:T(8,128)}, f32[1024,256]{1,0:T(8,128)}, f32[1024,256]{1,0:T(8,128)}, f32[256,1024]{1,0:T(8,128)}, f32[1024...) async-done(((f32[1024,256]{1,0:T(8,128)}, f32[1024,256]{1,0:T(8,128)}, f32[1024,256]{1,0:T(8,128)}, f32[256,1024]{1,0:T(8,128)}, f32[1024,1024]{1,0:T(8,128)}, ...) | async-done | bytes 16777232 | tf_op jit(solution)/shard_map/psum | solution.py:264
  (285 shorter events, 333.5 us)
Async XLA Ops:
  7.2 280.6 %copy-start = (bf16[1024,1024]{1,0:T(8,128)(2,1)S(1)}, bf16[1024,1024]{1,0:T(8,128)(2,1)}, u32[]{:S(2)}) copy-start(bf16[1024,1024]{1,0:T(8,128)(2,1)} %param.30) | copy-start | bytes 6291460
  7.2 43.9 %copy-start.30 = (bf16[1024,256]{1,0:T(8,128)(2,1)S(1)}, bf16[1024,256]{1,0:T(8,128)(2,1)}, u32[]{:S(2)}) copy-start(bf16[1024,256]{1,0:T(8,128)(2,1)} %param.23) | copy-start | bytes 1572868
  7.2 43.9 %all-gather.5.cloned.1.call-start = ((), (), s32[]{:S(2)}) async-start(), calls=%async_computation.4 | async-start | bytes 5242880 | tf_op jit(solution)/shard_map/all_gather | solution.py:98
  13.8 198.6 %reduce-scatter.5.cloned.1.call-start = ((), (), s32[]{:S(2)}) async-start(), calls=%async_computation.5 | async-start | bytes 10485760 | tf_op jit(solution)/shard_map/reduce_scatter | solution.py:146
  140.9 75.0 %copy-start.36 = (f32[1024]{0:T(1024)S(1)}, f32[1024]{0:T(1024)}, u32[]{:S(2)}) copy-start(f32[1024]{0:T(1024)} %param.26) | copy-start | bytes 12292
  140.9 75.0 %copy-start.42 = (f32[1024]{0:T(1024)S(1)}, f32[1024]{0:T(1024)}, u32[]{:S(2)}) copy-start(f32[1024]{0:T(1024)} %param.27) | copy-start | bytes 12292
  140.9 111.0 %all-gather.7.cloned.1.call-start = ((), (), s32[]{:S(2)}) async-start(), calls=%async_computation.6 | async-start | bytes 5242880 | tf_op jit(solution)/shard_map/all_gather | solution.py:154
  217.3 70.5 %all-gather.9.cloned.1.call-start = ((), (), s32[]{:S(2)}) async-start(), calls=%async_computation.8 | async-start | bytes 5242880 | tf_op jit(solution)/shard_map/all_gather | solution.py:169
  217.9 171.3 %reduce-scatter.9.cloned.1.call-start = ((), (), s32[]{:S(2)}) async-start(), calls=%async_computation.9 | async-start | bytes 10485760 | tf_op jit(solution)/shard_map/reduce_scatter | solution.py:178
  317.6 118.6 %reduce-scatter.7.cloned.1.call-start = ((), (), s32[]{:S(2)}) async-start(), calls=%async_computation.7 | async-start | bytes 5242880 | tf_op jit(solution)/shard_map/reduce_scatter | solution.py:161
  326.1 63.1 %copy-start.6 = (f32[512,1024]{1,0:T(8,128)S(1)}, f32[512,1024]{1,0:T(8,128)}, u32[]{:S(2)}) copy-start(f32[512,1024]{1,0:T(8,128)} %copy-done.5) | copy-start | bytes 6291460
  326.1 149.8 %all-gather.11.cloned.1.call-start = ((), (), s32[]{:S(2)}) async-start(), calls=%async_computation.10 | async-start | bytes 5242880 | tf_op jit(solution)/shard_map/all_gather | solution.py:188
  441.3 39.2 %copy-start.9 = (bf16[2048,4,64]{0,2,1:T(8,128)(2,1)S(1)}, bf16[2048,4,64]{0,2,1:T(8,128)(2,1)}, u32[]{:S(2)}) copy-start(bf16[2048,4,64]{0,2,1:T(8,128)(2,1)} %get-tuple-element.517) | copy-start | bytes 3145732
  441.3 480.7 %reduce-scatter.11.cloned.1.call-start = ((), (), s32[]{:S(2)}) async-start(), calls=%async_computation.11 | async-start | bytes 10485760 | tf_op jit(solution)/shard_map/reduce_scatter | solution.py:248
  528.5 38.4 %copy-start.4 = (bf16[2048,4,64]{0,2,1:T(8,128)(2,1)S(1)}, bf16[2048,4,64]{0,2,1:T(8,128)(2,1)}, u32[]{:S(2)}) copy-start(bf16[2048,4,64]{0,2,1:T(8,128)(2,1)} %copy-done.3) | copy-start | bytes 3145732 | tf_op jit(solution)/shard_map/while
  616.2 39.0 %copy-start.4 = (bf16[2048,4,64]{0,2,1:T(8,128)(2,1)S(1)}, bf16[2048,4,64]{0,2,1:T(8,128)(2,1)}, u32[]{:S(2)}) copy-start(bf16[2048,4,64]{0,2,1:T(8,128)(2,1)} %copy-done.3) | copy-start | bytes 3145732 | tf_op jit(solution)/shard_map/while
  704.4 39.0 %copy-start.4 = (bf16[2048,4,64]{0,2,1:T(8,128)(2,1)S(1)}, bf16[2048,4,64]{0,2,1:T(8,128)(2,1)}, u32[]{:S(2)}) copy-start(bf16[2048,4,64]{0,2,1:T(8,128)(2,1)} %copy-done.3) | copy-start | bytes 3145732 | tf_op jit(solution)/shard_map/while
  792.5 39.0 %copy-start.4 = (bf16[2048,4,64]{0,2,1:T(8,128)(2,1)S(1)}, bf16[2048,4,64]{0,2,1:T(8,128)(2,1)}, u32[]{:S(2)}) copy-start(bf16[2048,4,64]{0,2,1:T(8,128)(2,1)} %copy-done.3) | copy-start | bytes 3145732 | tf_op jit(solution)/shard_map/while
  850.5 589.5 %all-reduce.4.cloned.1.call-start = ((), (), s32[]{:S(2)}) async-start(), calls=%async_computation.12 | async-start | bytes 33554432 | tf_op jit(solution)/shard_map/psum | solution.py:264
  883.7 38.3 %copy-start.35 = (f32[512]{0:T(512)S(1)}, f32[512]{0:T(512)}, u32[]{:S(2)}) copy-start(f32[512]{0:T(512)} %copy-done.34) | copy-start | bytes 6148
  883.7 38.3 %copy-start.37 = (f32[1024]{0:T(1024)S(1)}, f32[1024]{0:T(1024)}, u32[]{:S(2)}) copy-start(f32[1024]{0:T(1024)} %param.20) | copy-start | bytes 12292
  883.7 38.3 %copy-start.39 = (f32[512]{0:T(512)S(1)}, f32[512]{0:T(512)}, u32[]{:S(2)}) copy-start(f32[512]{0:T(512)} %copy-done.38) | copy-start | bytes 6148
  883.7 40.9 %copy-start.40 = (f32[1024]{0:T(1024)S(1)}, f32[1024]{0:T(1024)}, u32[]{:S(2)}) copy-start(f32[1024]{0:T(1024)} %get-tuple-element.169) | copy-start | bytes 12292
  883.8 40.9 %copy-start.41 = (f32[1024]{0:T(1024)S(1)}, f32[1024]{0:T(1024)}, u32[]{:S(2)}) copy-start(f32[1024]{0:T(1024)} %get-tuple-element.175) | copy-start | bytes 12292
  (51 other events, 303.1 us)
Sparse Core Ops, SparseCore 0:
  13.9 37.1 all-gather.4
  141.0 71.3 reduce-scatter.4
  217.4 34.4 all-gather.6
  253.3 34.4 all-gather.8
  317.7 71.4 reduce-scatter.8
  391.5 44.5 reduce-scatter.6
  441.4 34.4 all-gather.10
  850.6 71.3 reduce-scatter.10
  929.0 511.0 all-reduce.3
where the time goes:
time: 1470 us; the launch traced here: 1460 us
  waiting for transfers between devices  803 us (55%)
  matrix products  441 us (30%)
  local copies, waits for them, and re-layouts  85.6 us (6%)
  other arithmetic  57.5 us (4%)
  blocking collectives  45 us (3%)
  loops' own time  15.4 us (1%)
    psum x1, waiting for transfers between devices, per_device(): lax.psum((grad_query_w, grad_key_w, grad_value_w, grad_output_w, grad_gat...  466 us
    dot_general x4, matrix products, backward_block(): jnp.einsum('hqk,qhd->khd', grad_raw, query_block, preferred_element_type=...  105 us
    dot_general x4, matrix products, backward_block(): jnp.einsum('hqk,khd->qhd', grad_raw, key_block, preferred_element_type=jn...  97.5 us
    reduce_scatter x1, waiting for transfers between devices, per_device(): lax.psum_scatter(jnp.dot(head_out, output_weight, preferred_element_type=...  71.5 us
    reduce_scatter x1, waiting for transfers between devices, per_device(): lax.psum_scatter(contract_cols(grad_gate, gate_weight) + contract_cols(gr...  63 us
    dynamic_update_slice x8, local copies, waits for them, and re-layouts, per_device(): lax.scan(backward_block, (zero_acc, zero_acc), (block_starts, log_totals))  50.7 us
    psum x1, blocking collectives, per_device(): lax.psum((attn_gain_part, attn_shift_part, mlp_gain_part, mlp_shift_part)...  45 us
    reduce_scatter x1, waiting for transfers between devices, per_device(): lax.psum_scatter(jnp.dot(hidden, down_weight, preferred_element_type=jnp....  43.9 us
  transfers between devices with their start and end apart: 9, of which 9 were waited for; matrix products, arithmetic and copies ran while one was open for 5% of the time, Pallas kernels for 0%

commit v1 on v0

v1 whole, which is shorter than its diff:
```python
import functools
import jax
import jax.numpy as jnp
from jax import lax
from jax.experimental import pallas as pl
from jax.experimental.pallas import tpu as pltpu
from jax.sharding import PartitionSpec as P

HEAD_DIM = 64
QT = 128
KT = 256
LANES = 128

epsilon = 1e-05


def nn(left, right):
    return lax.dot_general(left, right, (((1,), (0,)), ((), ())), preferred_element_type=jnp.float32)


def nt(left, right):
    return lax.dot_general(left, right, (((1,), (1,)), ((), ())), preferred_element_type=jnp.float32)


def tn(left, right):
    return lax.dot_general(left, right, (((0,), (0,)), ((), ())), preferred_element_type=jnp.float32)


def both_heads(block):
    lane = lax.broadcasted_iota(jnp.int32, block.shape, 1)
    zero = jnp.zeros_like(block)
    return jnp.concatenate([jnp.where(lane < HEAD_DIM, block, zero), jnp.where(lane >= HEAD_DIM, block, zero)], axis=0)


def own_blocks(wide):
    return jnp.concatenate([wide[:HEAD_DIM, :QT], wide[HEAD_DIM:, QT:]], axis=0)


def attend_kernel(first_ref, last_ref, q_ref, k_ref, v_ref, mark_ref, penalty_ref, head_ref, wide_ref, log_ref, score_ref, acc_ref, aug_ref):
    pairs = q_ref.shape[1] // LANES
    blocks = q_ref.shape[0] // QT
    for pair in range(pairs):
        aug_ref[pair, :, :LANES] = k_ref[:, pair * LANES:(pair + 1) * LANES]
        aug_ref[pair, :, LANES:] = mark_ref[...]

    def query_block(i, carry):
        rows = pl.ds(pl.multiple_of(i * QT, QT), QT)
        low, high = first_ref[i], last_ref[i]
        penalty = penalty_ref[rows, :]
        penalty = jnp.concatenate([penalty, penalty], axis=0)
        queries = [
            jnp.concatenate([both_heads(q_ref[rows, p * LANES:(p + 1) * LANES]), penalty], axis=1)
            for p in range(pairs)
        ]

        def first_pass(j, best):
            keys = pl.ds(pl.multiple_of(j * KT, KT), KT)
            out = []
            for p in range(pairs):
                scores = nt(aug_ref[p, keys, :], queries[p])
                score_ref[p, pl.ds(pl.multiple_of((j - low) * KT, KT), KT), :] = scores
                out.append(jnp.maximum(best[p], jnp.max(scores.reshape(KT // 8, 8, 2 * QT), axis=0)))
            return tuple(out)

        start = tuple(jnp.full((8, 2 * QT), -3e38, jnp.float32) for _ in range(pairs))
        best = lax.fori_loop(low, high, first_pass, start)
        best = [jnp.max(b, axis=0, keepdims=True) for b in best]
        acc_ref[...] = jnp.zeros_like(acc_ref)

        def second_pass(j, total):
            keys = pl.ds(pl.multiple_of(j * KT, KT), KT)
            out = []
            for p in range(pairs):
                scores = score_ref[p, pl.ds(pl.multiple_of((j - low) * KT, KT), KT), :]
                weight = jnp.exp(scores - best[p])
                out.append(total[p] + jnp.sum(weight.reshape(KT // 8, 8, 2 * QT), axis=0))
                acc_ref[p] += tn(v_ref[keys, p * LANES:(p + 1) * LANES], weight.astype(jnp.bfloat16))
            return tuple(out)

        zero = tuple(jnp.zeros((8, 2 * QT), jnp.float32) for _ in range(pairs))
        total = lax.fori_loop(low, high, second_pass, zero)
        for p in range(pairs):
            denom = jnp.sum(total[p], axis=0, keepdims=True)
            log_total = best[p] + jnp.log(denom)
            log_ref[2 * p:2 * p + 1, rows] = log_total[:, :QT]
            log_ref[2 * p + 1:2 * p + 2, rows] = log_total[:, QT:]
            mixed = own_blocks(acc_ref[p] / denom).T
            wide_ref[rows, p * LANES:(p + 1) * LANES] = mixed
            head_ref[rows, p * LANES:(p + 1) * LANES] = mixed.astype(jnp.bfloat16)
        return carry

    lax.fori_loop(0, blocks, query_block, 0)


def vmem():
    return pl.BlockSpec(memory_space=pltpu.VMEM)


def smem():
    return pl.BlockSpec(memory_space=pltpu.SMEM)


def cost(flops, moved):
    return pl.CostEstimate(flops=flops, bytes_accessed=moved, transcendentals=0)


def attend(first, last, q, k, v, mark, penalty):
    tokens, width = q.shape
    pairs = width // LANES
    return pl.pallas_call(
        attend_kernel,
        out_shape=(
            jax.ShapeDtypeStruct((tokens, width), jnp.bfloat16),
            jax.ShapeDtypeStruct((tokens, width), jnp.float32),
            jax.ShapeDtypeStruct((2 * pairs, tokens), jnp.float32),
        ),
        in_specs=[smem(), smem()] + [vmem()] * 5,
        out_specs=(vmem(), vmem(), vmem()),
        scratch_shapes=[
            pltpu.VMEM((pairs, tokens, 2 * QT), jnp.float32),
            pltpu.VMEM((pairs, LANES, 2 * QT), jnp.float32),
            pltpu.VMEM((pairs, tokens, 2 * LANES), jnp.bfloat16),
        ],
        name="attend",
        cost_estimate=pl.CostEstimate(flops=2 * 10**9, bytes_accessed=8 * 2**20, transcendentals=0),
    )(first, last, q, k, v, mark, penalty)


def turn(values):
    lane = lax.broadcasted_iota(jnp.int32, values.shape, 1)
    quarter = HEAD_DIM // 2
    ahead = pltpu.roll(values, LANES - quarter, 1)
    behind = pltpu.roll(values, quarter, 1)
    return jnp.where(lane % HEAD_DIM < quarter, ahead, behind)


def attend_back_kernel(first_ref, last_ref, q_ref, k_ref, v_ref, mark_ref, penalty_ref, wide_ref, log_ref, cot_ref, cos_ref, sin_ref,
                       dq_ref, dk_ref, dv_ref, aug_ref, dkey_ref, dval_ref, dqry_ref):
    pairs = q_ref.shape[1] // LANES
    blocks = q_ref.shape[0] // QT
    for pair in range(pairs):
        aug_ref[pair, :, :LANES] = k_ref[:, pair * LANES:(pair + 1) * LANES]
        aug_ref[pair, :, LANES:] = mark_ref[...]
    dkey_ref[...] = jnp.zeros_like(dkey_ref)
    dval_ref[...] = jnp.zeros_like(dval_ref)

    def query_block(i, carry):
        rows = pl.ds(pl.multiple_of(i * QT, QT), QT)
        low, high = first_ref[i], last_ref[i]
        penalty = penalty_ref[rows, :]
        penalty = jnp.concatenate([penalty, penalty], axis=0)
        plain, queries, cots, logs, deltas = [], [], [], [], []
        for p in range(pairs):
            lanes = slice(p * LANES, (p + 1) * LANES)
            block = both_heads(q_ref[rows, lanes])
            plain.append(block)
            queries.append(jnp.concatenate([block, penalty], axis=1))
            cot = cot_ref[rows, lanes]
            cots.append(both_heads(cot))
            product = (cot.astype(jnp.float32) * wide_ref[rows, lanes]).T
            deltas.append(jnp.concatenate(
                [jnp.sum(product[:HEAD_DIM], axis=0, keepdims=True), jnp.sum(product[HEAD_DIM:], axis=0, keepdims=True)], axis=1))
            logs.append(jnp.concatenate([log_ref[2 * p:2 * p + 1, rows], log_ref[2 * p + 1:2 * p + 2, rows]], axis=1))
        dqry_ref[...] = jnp.zeros_like(dqry_ref)

        def key_block(j, inner):
            keys = pl.ds(pl.multiple_of(j * KT, KT), KT)
            for p in range(pairs):
                lanes = slice(p * LANES, (p + 1) * LANES)
                prob = jnp.exp(nt(aug_ref[p, keys, :], queries[p]) - logs[p])
                grad_prob = nt(v_ref[keys, lanes], cots[p])
                grad_raw = (prob * (grad_prob - deltas[p])).astype(jnp.bfloat16)
                dval_ref[keys, lanes] += nn(prob.astype(jnp.bfloat16), cots[p])
                dkey_ref[keys, lanes] += nn(grad_raw, plain[p])
                dqry_ref[p] += tn(k_ref[keys, lanes], grad_raw)
            return inner

        lax.fori_loop(low, high, key_block, 0)
        cosine, sine = cos_ref[rows, :], sin_ref[rows, :]
        for p in range(pairs):
            grad = own_blocks(dqry_ref[p]).T * (HEAD_DIM ** -0.5)
            dq_ref[rows, p * LANES:(p + 1) * LANES] = (grad * cosine - turn(grad) * sine).astype(jnp.bfloat16)
        return carry

    lax.fori_loop(0, blocks, query_block, 0)

    def finish(i, carry):
        rows = pl.ds(pl.multiple_of(i * QT, QT), QT)
        cosine, sine = cos_ref[rows, :], sin_ref[rows, :]
        for p in range(pairs):
            lanes = slice(p * LANES, (p + 1) * LANES)
            grad = dkey_ref[rows, lanes]
            dk_ref[rows, lanes] = (grad * cosine - turn(grad) * sine).astype(jnp.bfloat16)
            dv_ref[rows, lanes] = dval_ref[rows, lanes].astype(jnp.bfloat16)
        return carry

    lax.fori_loop(0, blocks, finish, 0)


def attend_back(first, last, q, k, v, mark, penalty, wide, logs, cot, cosine, sine):
    tokens, width = q.shape
    pairs = width // LANES
    out = jax.ShapeDtypeStruct((tokens, width), jnp.bfloat16)
    return pl.pallas_call(
        attend_back_kernel,
        out_shape=(out, out, out),
        in_specs=[smem(), smem()] + [vmem()] * 10,
        out_specs=(vmem(),) * 3,
        scratch_shapes=[
            pltpu.VMEM((pairs, tokens, 2 * LANES), jnp.bfloat16),
            pltpu.VMEM((tokens, width), jnp.float32),
            pltpu.VMEM((tokens, width), jnp.float32),
            pltpu.VMEM((pairs, LANES, 2 * QT), jnp.float32),
        ],
        name="attend_back",
        cost_estimate=pl.CostEstimate(flops=5 * 10**9, bytes_accessed=16 * 2**20, transcendentals=0),
    )(first, last, q, k, v, mark, penalty, wide, logs, cot, cosine, sine)


def swap(values, bit, axis="mp"):
    size = lax.axis_size(axis)
    return lax.ppermute(values, axis, [(i, i ^ bit) for i in range(size)])


def gather_pieces(own):
    across = swap(own, 2)
    beside = swap(own, 1)
    return [own, beside, across, swap(across, 1)]


def scatter_sum(term, after=None):
    far = swap(term(3), 1)
    pair = (term(2).astype(jnp.float32) + far.astype(jnp.float32)).astype(jnp.bfloat16)
    if after is not None:
        pair, _ = lax.optimization_barrier((pair, after))
    cross = swap(pair, 2)
    near = swap(term(1), 1)
    return term(0).astype(jnp.float32) + near.astype(jnp.float32) + cross.astype(jnp.float32)


def reduce_dp(values, order):
    place = lax.axis_index("dp")
    bits = []
    while 1 << len(bits) < lax.axis_size("dp"):
        bits.append(1 << len(bits))
    bits = bits[order:] + bits[:order]
    for bit in bits:
        half = values.shape[0] // 2
        high = lax.bitwise_and(place, bit) // bit
        keep = lax.dynamic_slice_in_dim(values, high * half, half, 0)
        send = lax.dynamic_slice_in_dim(values, (1 - high) * half, half, 0)
        got = swap(send, bit, "dp")
        values = (keep.astype(jnp.float32) + got.astype(jnp.float32)).astype(jnp.bfloat16)
    for bit in reversed(bits):
        high = lax.bitwise_and(place, bit)
        other = swap(values, bit, "dp")
        values = jnp.where(high == 0, jnp.concatenate([values, other]), jnp.concatenate([other, values]))
    return values


def sum_all(values):
    for axis in ("mp", "dp"):
        bit = 1
        while bit < lax.axis_size(axis):
            values = values + swap(values, bit, axis)
            bit *= 2
    return values


def place_of(index_ref, j, rows):
    return pl.ds(pl.multiple_of(lax.bitwise_xor(index_ref[0], j) * rows, rows), rows)


def project_kernel(index_ref, a_ref, b_ref, c_ref, d_ref, weight_ref, cos_ref, sin_ref, q_ref, k_ref, v_ref):
    rows = a_ref.shape[0]
    width = q_ref.shape[1]
    for j, piece in enumerate((a_ref, b_ref, c_ref, d_ref)):
        place = place_of(index_ref, j, rows)
        cosine, sine = cos_ref[place, :], sin_ref[place, :]
        product = nn(piece[...], weight_ref[...])
        for out, base, scale in ((q_ref, 0, HEAD_DIM**-0.5), (k_ref, width, None)):
            for p in range(width // LANES):
                part = product[:, base + p * LANES : base + (p + 1) * LANES]
                turned = part * cosine + turn(part) * sine
                if scale is not None:
                    turned = turned * scale
                out[place, p * LANES : (p + 1) * LANES] = turned.astype(jnp.bfloat16)
        v_ref[place, :] = product[:, 2 * width :].astype(jnp.bfloat16)


def project(index, pieces, weight, cosine, sine):
    tokens = cosine.shape[0]
    width = weight.shape[1] // 3
    out = jax.ShapeDtypeStruct((tokens, width), jnp.bfloat16)
    return pl.pallas_call(
        project_kernel,
        out_shape=(out, out, out),
        in_specs=[smem()] + [vmem()] * 7,
        out_specs=(vmem(),) * 3,
        name="project",
        cost_estimate=cost(2 * tokens * weight.shape[0] * weight.shape[1], 10 * 2**20),
    )(index, *pieces, weight, cosine, sine)


def head_back_kernel(index_ref, a_ref, b_ref, c_ref, d_ref, weight_ref, out_ref):
    rows = a_ref.shape[0]
    for j, piece in enumerate((a_ref, b_ref, c_ref, d_ref)):
        out_ref[place_of(index_ref, j, rows), :] = nt(piece[...], weight_ref[...]).astype(jnp.bfloat16)


def head_back(index, pieces, weight):
    tokens = 4 * pieces[0].shape[0]
    return pl.pallas_call(
        head_back_kernel,
        out_shape=jax.ShapeDtypeStruct((tokens, weight.shape[0]), jnp.bfloat16),
        in_specs=[smem()] + [vmem()] * 5,
        out_specs=vmem(),
        name="head_back",
        cost_estimate=cost(2 * tokens * weight.shape[0] * weight.shape[1], 6 * 2**20),
    )(index, *pieces, weight)


def weight_grad_kernel(many, index_ref, *refs):
    lefts, rights = refs[: many[0]], [refs[many[0] + many[1] * r : many[0] + many[1] * (r + 1)] for r in range(many[2])]
    outs = refs[many[0] + many[1] * many[2] :]
    rows = lefts[0].shape[0] if many[0] == 4 else lefts[0].shape[0] // 4
    totals = [None] * len(rights)
    for j in range(4):
        place = place_of(index_ref, j, rows)
        left = lefts[j][...] if many[0] == 4 else lefts[0][place, :]
        for n, right in enumerate(rights):
            part = tn(left, right[j][...] if many[1] == 4 else right[0][place, :])
            totals[n] = part if totals[n] is None else totals[n] + part
    if len(outs) == 1:
        outs[0][...] = jnp.concatenate(totals, axis=1).astype(jnp.bfloat16)
    else:
        for out, total in zip(outs, totals):
            out[...] = total.astype(jnp.bfloat16)


def weight_grad(index, lefts, rights, tile, join=False):
    many = (len(lefts), len(rights[0]), len(rights))
    left_rows, depth = lefts[0].shape
    flat = [array for right in rights for array in right]
    wide = sum(right[0].shape[1] for right in rights)
    outs = tuple(jax.ShapeDtypeStruct((depth, right[0].shape[1]), jnp.bfloat16) for right in rights)
    if join:
        outs = (jax.ShapeDtypeStruct((depth, wide), jnp.bfloat16),)
    tokens = left_rows * (4 // len(lefts))
    return pl.pallas_call(
        functools.partial(weight_grad_kernel, many),
        grid=(depth // tile,),
        out_shape=outs,
        in_specs=[smem()]
        + [pl.BlockSpec((left_rows, tile), lambda i: (0, i))] * len(lefts)
        + [pl.BlockSpec(array.shape, lambda i: (0, 0)) for array in flat],
        out_specs=tuple(pl.BlockSpec((tile, o.shape[1]), lambda i: (i, 0)) for o in outs),
        cost_estimate=cost(2 * tokens * depth * wide, 2 * (tokens * (depth + wide) + depth * wide)),
    )(index, *lefts, *flat)


def spread_kernel(count, flip, targets, index_ref, *refs):
    arrays, weights, outs = refs[:count], refs[count : 2 * count], refs[2 * count :]
    rows = arrays[0].shape[0] // 4
    product = nt if flip else nn
    for out, j in zip(outs, targets):
        place = place_of(index_ref, j, rows)
        total = product(arrays[0][place, :], weights[0][...])
        for array, weight in zip(arrays[1:], weights[1:]):
            total = total + product(array[place, :], weight[...])
        out[...] = total.astype(jnp.bfloat16)


def spread(index, arrays, weights, flip, targets):
    tokens, depth = arrays[0].shape
    width = weights[0].shape[0 if flip else 1]
    count = len(arrays)
    out = jax.ShapeDtypeStruct((tokens // 4, width), jnp.bfloat16)
    return pl.pallas_call(
        functools.partial(spread_kernel, count, flip, targets),
        out_shape=(out,) * len(targets),
        in_specs=[smem()] + [vmem()] * (2 * count),
        out_specs=(vmem(),) * len(targets),
        cost_estimate=cost(2 * count * len(targets) * (tokens // 4) * depth * width, 2 * 2**20 * len(targets)),
    )(index, *arrays, *weights)


def feed_kernel(count, *refs):
    inputs, cots = refs[:count], refs[count : 2 * count]
    gate_w, up_w, down_w = refs[2 * count : 2 * count + 3]
    outs = refs[2 * count + 3 :]
    for j in range(count):
        normed = inputs[j][...]
        gate = nn(normed, gate_w[...])
        up = nn(normed, up_w[...])
        grad = nt(cots[j][...], down_w[...])
        sig = jax.nn.sigmoid(gate)
        silu = gate * sig
        outs[j][...] = (silu * up).astype(jnp.bfloat16)
        outs[count + j][...] = (grad * up * (sig + silu * (1.0 - sig))).astype(jnp.bfloat16)
        outs[2 * count + j][...] = (grad * silu).astype(jnp.bfloat16)


def feed(inputs, cots, gate_w, up_w, down_w, tile=256):
    count = len(inputs)
    rows, width = inputs[0].shape
    hidden = gate_w.shape[1]
    out = jax.ShapeDtypeStruct((rows, hidden), jnp.bfloat16)
    whole = pl.BlockSpec((rows, width), lambda i: (0, 0))
    column = pl.BlockSpec((width, tile), lambda i: (0, i))
    outs = pl.pallas_call(
        functools.partial(feed_kernel, count),
        grid=(hidden // tile,),
        out_shape=(out,) * (3 * count),
        in_specs=[whole] * (2 * count) + [column, column, pl.BlockSpec((tile, width), lambda i: (i, 0))],
        out_specs=(pl.BlockSpec((rows, tile), lambda i: (0, i)),) * (3 * count),
        name="feed",
        cost_estimate=cost(6 * count * rows * width * hidden, 2 * (3 * width * hidden + count * rows * (2 * width + 3 * hidden))),
    )(*inputs, *cots, gate_w, up_w, down_w)
    return outs[:count], outs[count : 2 * count], outs[2 * count :]


def normalize(values):
    center = values - jnp.mean(values, axis=-1, keepdims=True)
    inverse = lax.rsqrt(jnp.mean(center * center, axis=-1, keepdims=True) + epsilon)
    return (center * inverse, inverse)


def norm_back(incoming, scaled, inverse, gain):
    gain_part = jnp.sum(incoming * scaled, axis=0)
    shift_part = jnp.sum(incoming, axis=0)
    along = incoming * gain
    mean_plain = jnp.mean(along, axis=-1, keepdims=True)
    mean_mixed = jnp.mean(along * scaled, axis=-1, keepdims=True)
    return (inverse * (along - mean_plain - scaled * mean_mixed), gain_part, shift_part)


def window_plan(seg):
    tokens = seg.shape[0]
    heads = seg[::QT]
    tails = seg[QT - 1 :: QT]
    begin = jnp.sum((seg[None, :] < heads[:, None]).astype(jnp.int32), axis=1)
    end = jnp.sum((seg[None, :] <= tails[:, None]).astype(jnp.int32), axis=1)
    first = begin // KT
    last = (end + KT - 1) // KT
    number = lax.broadcasted_iota(jnp.int32, (tokens, LANES), 1)
    same = seg[:, None] == number
    mark = same.astype(jnp.bfloat16)
    penalty = jnp.where(same, 0.0, -1e30).astype(jnp.bfloat16)
    opening = jnp.sum((seg[:, None] < number).astype(jnp.int32), axis=0)
    start = jnp.sum(jnp.where(same, opening[None, :], 0), axis=1)
    position = (jnp.arange(tokens, dtype=jnp.int32) - start).astype(jnp.float32)
    half_dim = HEAD_DIM // 2
    frequency = 10000.0 ** (-2.0 * jnp.arange(half_dim, dtype=jnp.float32) / HEAD_DIM)
    angles = position[:, None] * jnp.tile(frequency, LANES // half_dim)[None, :]
    sign = jnp.where(jnp.arange(LANES) % HEAD_DIM < half_dim, -1.0, 1.0)
    cosine, sine = jnp.cos(angles), jnp.sin(angles) * sign[None, :]
    return first, last, mark, penalty, cosine, sine


def layer(
    tokens,
    segments,
    attn_norm_gain,
    attn_norm_bias,
    query_weight,
    key_weight,
    value_weight,
    output_weight,
    mlp_norm_gain,
    mlp_norm_bias,
    gate_weight,
    up_weight,
    down_weight,
    grad_out,
):
    position = lax.axis_index("mp")
    index = position.astype(jnp.int32).reshape(1)
    first, last, mark, penalty, cosine, sine = window_plan(segments.reshape(-1))

    inputs = tokens.astype(jnp.float32)
    attn_scaled, attn_inverse = normalize(inputs)
    attn_normed = (attn_scaled * attn_norm_gain + attn_norm_bias).astype(jnp.bfloat16)
    attn_pieces = gather_pieces(attn_normed)
    qkv_weight = jnp.concatenate([query_weight, key_weight, value_weight], axis=1)
    query_rot, key_rot, value_low = project(index, attn_pieces, qkv_weight, cosine, sine)
    late_cot, _ = lax.optimization_barrier((grad_out, attn_pieces[2]))
    cot_pieces = gather_pieces(late_cot)
    head_out, head_wide, log_totals = attend(first, last, query_rot, key_rot, value_low, mark, penalty)
    outward = spread(index, [head_out], [output_weight], False, (3, 2))
    inward = spread(index, [head_out], [output_weight], False, (1, 0))
    middle = inputs + scatter_sum([inward[1], inward[0], outward[1], outward[0]].__getitem__)
    mlp_scaled, mlp_inverse = normalize(middle)
    mlp_normed = (mlp_scaled * mlp_norm_gain + mlp_norm_bias).astype(jnp.bfloat16)
    mlp_pieces = gather_pieces(mlp_normed)
    near = feed(mlp_pieces[:2], cot_pieces[:2], gate_weight, up_weight, down_weight)
    far = feed(mlp_pieces[2:], cot_pieces[2:], gate_weight, up_weight, down_weight)
    hidden, grad_gate, grad_up = [list(a) + list(b) for a, b in zip(near, far)]
    grad_mlp_normed = scatter_sum(
        lambda j: (nt(grad_gate[j], gate_weight) + nt(grad_up[j], up_weight)).astype(jnp.bfloat16)
    )
    (grad_down,) = weight_grad(index, hidden, [cot_pieces], 256)
    grad_gate_w, grad_up_w = weight_grad(index, mlp_pieces, [grad_gate, grad_up], 256)
    summed_gate, summed_up, summed_down = lax.psum((grad_gate_w, grad_up_w, grad_down), "dp")
    middle_part, mlp_gain_part, mlp_shift_part = norm_back(grad_mlp_normed, mlp_scaled, mlp_inverse, mlp_norm_gain)
    grad_middle = grad_out.astype(jnp.float32) + middle_part
    attn_cot = gather_pieces(grad_middle.astype(jnp.bfloat16))
    grad_head = head_back(index, attn_cot, output_weight)
    block_out = (
        middle
        + scatter_sum(
            lambda j: jnp.dot(hidden[j], down_weight, preferred_element_type=jnp.float32).astype(jnp.bfloat16),
            attn_cot[2],
        )
    ).astype(jnp.bfloat16)
    (grad_output_w,) = weight_grad(index, attn_cot, [[head_out]], 256, True)
    grad_query, grad_key, grad_value = attend_back(
        first, last, query_rot, key_rot, value_low, mark, penalty, head_wide, log_totals, grad_head, cosine, sine
    )
    first_part, second_part = weight_grad(
        index, attn_pieces, [[grad_query], [grad_key], [grad_value]], 256, True
    )[0], grad_output_w
    width = grad_query.shape[1]
    second_part = jnp.concatenate([first_part[:, 2 * width :], second_part], axis=1)
    first_part = reduce_dp(first_part[:, : 2 * width], 0)
    second_part = reduce_dp(second_part, 1)
    qkv = [grad_query, grad_key, grad_value], [query_weight, key_weight, value_weight]
    outward = spread(index, *qkv, True, (3, 2))
    inward = spread(index, *qkv, True, (1, 0))
    grad_attn_normed = scatter_sum([inward[1], inward[0], outward[1], outward[0]].__getitem__)
    input_part, attn_gain_part, attn_shift_part = norm_back(grad_attn_normed, attn_scaled, attn_inverse, attn_norm_gain)
    grad_tokens = grad_middle + input_part
    sums = sum_all(jnp.stack([attn_gain_part, attn_shift_part, mlp_gain_part, mlp_shift_part]))

    def wide(values):
        return values.astype(jnp.float32)

    return (
        block_out,
        grad_tokens,
        sums[0],
        sums[1],
        wide(first_part[:, :width]),
        wide(first_part[:, width:]),
        wide(second_part[:, :width]),
        wide(second_part[:, width:].T),
        sums[2],
        sums[3],
        wide(summed_gate),
        wide(summed_up),
        wide(summed_down),
    )


def solution(mesh):
    in_specs = (
        P(("dp", "mp"), None),
        P("dp", None),
        P(),
        P(),
        P(None, "mp"),
        P(None, "mp"),
        P(None, "mp"),
        P("mp", None),
        P(),
        P(),
        P(None, "mp"),
        P(None, "mp"),
        P("mp", None),
        P(("dp", "mp"), None),
    )
    out_specs = (
        P(("dp", "mp"), None),
        P(("dp", "mp"), None),
        P(),
        P(),
        P(None, "mp"),
        P(None, "mp"),
        P(None, "mp"),
        P("mp", None),
        P(),
        P(),
        P(None, "mp"),
        P(None, "mp"),
        P("mp", None),
    )
    return jax.shard_map(layer, mesh=mesh, in_specs=in_specs, out_specs=out_specs, check_vma=False)
```

time: 1470 us -> 589 us (0.40)
  waiting for transfers between devices: 803 us -> 281 us
  matrix products: 441 us -> 29.9 us
  Pallas kernels: 0 us -> 159 us
  local copies, waits for them, and re-layouts: 85.6 us -> 8.87 us
  blocking collectives: 45 us -> 0 us
  starting transfers between devices: 0.37 us -> 36.6 us
  loops' own time: 15.4 us -> 0 us
    psum x1, waiting for transfers between devices: 466 us -> 0.01 us  [layer(): lax.psum((grad_gate_w, grad_up_w, grad_down), 'dp')]
    dot_general x49 -> x12, matrix products: 441 us -> 29.9 us  [the longest x8 16.5 us: nt(): lax.dot_general(left, right, (((1,), (1,)), ((), ())), preferred_element_...]
    ppermute x0 -> x41, waiting for transfers between devices: none -> 281 us  [swap(): return lax.ppermute(values, axis, [(i, i ^ bit) for i in range(size)])]
    reduce_scatter x4 -> x0, waiting for transfers between devices: 217 us -> none  [the longest x1 71.5 us: per_device(): lax.psum_scatter(jnp.dot(head_out, output_weight, preferred_element_type=...]
    pallas_call x0 -> x14, Pallas kernels: none -> 159 us  [the longest x1 42.4 us: attend_back(): pl.pallas_call(attend_back_kernel, out_shape=(out, out, out), in_specs=[s...]
    all_gather x4 -> x0, waiting for transfers between devices: 120 us -> none  [the longest x1 34.5 us: per_device(): lax.all_gather(grad_middle.astype(jnp.bfloat16), 'mp', axis=0, tiled=True)]
    dynamic_update_slice x8 -> x0, local copies, waits for them, and re-layouts: 50.7 us -> none  [per_device(): lax.scan(backward_block, (zero_acc, zero_acc), (block_starts, log_totals))]
    psum x1 -> x0, blocking collectives: 45 us -> none  [per_device(): lax.psum((attn_gain_part, attn_shift_part, mlp_gain_part, mlp_shift_part)...]
  transfers between devices with their start and end apart: 9 -> 42, of which waited for: 9 -> 18; matrix products, arithmetic and copies ran while one was open for 5% -> 13% of each run, Pallas kernels for 0% -> 18%
where the time goes in v1:
time: 589 us; the launch traced here: 585 us
  waiting for transfers between devices  281 us (48%)
  Pallas kernels  159 us (27%)
  other arithmetic  54.1 us (9%)
  starting transfers between devices  36.6 us (6%)
  matrix products  29.9 us (5%)
  between operations  14.9 us (3%)
  local copies, waits for them, and re-layouts  8.87 us (2%)
    ppermute x41, waiting for transfers between devices, swap(): return lax.ppermute(values, axis, [(i, i ^ bit) for i in range(size)])  281 us
    pallas_call x1, Pallas kernels, attend_back(): pl.pallas_call(attend_back_kernel, out_shape=(out, out, out), in_specs=[s...  42.4 us
    ppermute x41, starting transfers between devices, swap(): return lax.ppermute(values, axis, [(i, i ^ bit) for i in range(size)])  36.5 us
    pallas_call x4, Pallas kernels, weight_grad(): pl.pallas_call(functools.partial(weight_grad_kernel, many), grid=(depth /...  35.9 us
    pallas_call x1, Pallas kernels, attend(): pl.pallas_call(attend_kernel, out_shape=(jax.ShapeDtypeStruct((tokens, wi...  28.3 us
    pallas_call x2, Pallas kernels, feed(): pl.pallas_call(functools.partial(feed_kernel, count), grid=(hidden // til...  23.3 us
    dot_general x8, matrix products, nt(): lax.dot_general(left, right, (((1,), (1,)), ((), ())), preferred_element_...  16.5 us
    pallas_call x4, Pallas kernels, spread(): pl.pallas_call(functools.partial(spread_kernel, count, flip, targets), ou...  16.5 us
  transfers between devices with their start and end apart: 42, of which 18 were waited for; matrix products, arithmetic and copies ran while one was open for 13% of the time, Pallas kernels for 18%

profile of v1, /device:TPU:0, one launch (start us, length us, event | category | flops | bytes accessed | tf_op | source)
XLA Modules:
  0.0 584.9 jit_solution(7587794087013519507)
XLA Ops:
  19.8 17.4 %collective-permute-done.1.c_ref.refs_2_ = bf16[512,1024]{1,0:T(8,128)(2,1)S(1)} collective-permute-done((bf16[512,1024]{1,0:T(8,128)(2,1)S(1)}, bf16[512,1024]{1,0:T(8,128)(2,1)S(1)}, u32[]{:S(2)}, u32[]{:S(2)}) %collective-permute-start.1) | collective-permute-done | bytes 1048608 | tf_op jit(solution)/shard_map/ppermute | solution.py:222
  38.3 5.7 fusion.14
  45.0 8.4 %project.1 = (bf16[2048,256]{1,0:T(8,128)(2,1)}, bf16[2048,256]{1,0:T(8,128)(2,1)}, bf16[2048,256]{1,0:T(8,128)(2,1)}) custom-call(s32[1]{0:T(128)} %bitcast.index_ref, bf16[512,1024]{1,0:T(8,128)(2,1)} %copy-done.5, bf16[512,1024]{1,0:T(8,128)(2,1)} %collective-permute-done.b_ref.refs_1_, bf16[512,1024]{1,0:T(8,128)(2,1)} %copy-done.11, ...), custom_call_target="tpu_custom_call" | custom-call | flops 3221225472 | bytes 10485760 | tf_op jit(solution)/shard_map/project/pallas_call | solution.py:295
  53.4 28.3 %attend.1 = (bf16[2048,256]{1,0:T(8,128)(2,1)}, f32[2048,256]{1,0:T(8,128)}, f32[4,2048]{1,0:T(4,128)}) custom-call(s32[16]{0:T(128)} %get-tuple-element.134.first_ref, s32[16]{0:T(128)} %get-tuple-element.133.last_ref, bf16[2048,256]{1,0:T(8,128)(2,1)} %get-tuple-element.46.q_ref, bf16[2048,256]{1,0:T(8,128)(2,1)} %get-tuple-element.47.k_ref, ...), custom_call_target="tpu_custom_call" | custom-call | flops 2000000000 | bytes 8388608 | tf_op jit(solution)/shard_map/attend/pallas_call | solution.py:110
  91.4 23.7 %collective-permute-done.5 = bf16[512,1024]{1,0:T(8,128)(2,1)S(1)} collective-permute-done((bf16[512,1024]{1,0:T(8,128)(2,1)S(1)}, bf16[512,1024]{1,0:T(8,128)(2,1)S(1)}, u32[]{:S(2)}, u32[]{:S(2)}) %collective-permute-start.5) | collective-permute-done | bytes 1048608 | tf_op jit(solution)/shard_map/ppermute | solution.py:222
  119.2 18.5 %collective-permute-done.11.refs_2_.refs_6_ = bf16[512,1024]{1,0:T(8,128)(2,1)} collective-permute-done((bf16[512,1024]{1,0:T(8,128)(2,1)}, bf16[512,1024]{1,0:T(8,128)(2,1)}, u32[]{:S(2)}, u32[]{:S(2)}) %collective-permute-start.11) | collective-permute-done | bytes 1048608 | tf_op jit(solution)/shard_map/ppermute | solution.py:222
  137.7 21.9 %collective-permute-done.9.refs_0_.refs_2_ = bf16[512,1024]{1,0:T(8,128)(2,1)} collective-permute-done((bf16[512,1024]{1,0:T(8,128)(2,1)S(1)}, bf16[512,1024]{1,0:T(8,128)(2,1)}, u32[]{:S(2)}, u32[]{:S(2)}) %collective-permute-start.9) | collective-permute-done | bytes 1048608 | tf_op jit(solution)/shard_map/ppermute | solution.py:222
  159.7 11.6 %feed.2 = (bf16[512,1024]{1,0:T(8,128)(2,1)}, bf16[512,1024]{1,0:T(8,128)(2,1)}, bf16[512,1024]{1,0:T(8,128)(2,1)}, bf16[512,1024]{1,0:T(8,128)(2,1)}, bf16[512,...) custom-call(bf16[512,1024]{1,0:T(8,128)(2,1)} %copy-done.6, bf16[512,1024]{1,0:T(8,128)(2,1)} %collective-permute-done.6.refs_1_, ...), custom_call_target="tpu_custom_call" | custom-call | flops 6442450944 | bytes 16777216 | tf_op jit(solution)/shard_map/feed/pallas_call | solution.py:411
  175.8 11.7 %feed.3 = (bf16[512,1024]{1,0:T(8,128)(2,1)}, bf16[512,1024]{1,0:T(8,128)(2,1)}, bf16[512,1024]{1,0:T(8,128)(2,1)}, bf16[512,1024]{1,0:T(8,128)(2,1)}, bf16[512,...) custom-call(bf16[512,1024]{1,0:T(8,128)(2,1)} %collective-permute-done.9.refs_0_.refs_2_, ...), custom_call_target="tpu_custom_call" | custom-call | flops 6442450944 | bytes 16777216 | tf_op jit(solution)/shard_map/feed/pallas_call | solution.py:411
  200.9 22.5 %collective-permute-done.16 = bf16[512,1024]{1,0:T(8,128)(2,1)S(1)} collective-permute-done((bf16[512,1024]{1,0:T(8,128)(2,1)S(1)}, bf16[512,1024]{1,0:T(8,128)(2,1)S(1)}, u32[]{:S(2)}, u32[]{:S(2)}) %collective-permute-start.16) | collective-permute-done | bytes 1048608 | tf_op jit(solution)/shard_map/ppermute | solution.py:222
  236.2 18.4 %collective-permute-done.17.c_ref.refs_2_ = bf16[512,1024]{1,0:T(8,128)(2,1)} collective-permute-done((bf16[512,1024]{1,0:T(8,128)(2,1)}, bf16[512,1024]{1,0:T(8,128)(2,1)}, u32[]{:S(2)}, u32[]{:S(2)}) %collective-permute-start.17) | collective-permute-done | bytes 1048608 | tf_op jit(solution)/shard_map/ppermute | solution.py:222
  260.1 8.7 %shard_map.244 = bf16[1024,1024]{1,0:T(8,128)(2,1)} custom-call(s32[1]{0:T(128)} %bitcast.index_ref, bf16[512,1024]{1,0:T(8,128)(2,1)} %get-tuple-element.55.refs_0_, bf16[512,1024]{1,0:T(8,128)(2,1)} %get-tuple-element.56.refs_1_, bf16[512,1024]{1,0:T(8,128)(2,1)} %get-tuple-element.57.refs_2_, bf16[512,1024]{1,0:T(8,128)(2,1)} %get-tuple-element.58.refs_3_, ...), custom_call_target="tpu_custom_call" | custom-call | flops 1073741824 | bytes 4194304 | tf_op jit(solution)/shard_map/pallas_call | solution.py:350
  268.8 14.2 %shard_map.243 = (bf16[1024,1024]{1,0:T(8,128)(2,1)}, bf16[1024,1024]{1,0:T(8,128)(2,1)}) custom-call(s32[1]{0:T(128)} %bitcast.index_ref, bf16[512,1024]{1,0:T(8,128)(2,1)} %copy-done.6, bf16[512,1024]{1,0:T(8,128)(2,1)} %collective-permute-done.6.refs_1_, bf16[512,1024]{1,0:T(8,128)(2,1)} %collective-permute-done.9.refs_0_.refs_2_, ...), custom_call_target="tpu_custom_call" | custom-call | flops 2147483648 | bytes 7340032 | tf_op jit(solution)/shard_map/pallas_call | solution.py:350
  291.7 42.4 %attend_back.1 = (bf16[2048,256]{1,0:T(8,128)(2,1)}, bf16[2048,256]{1,0:T(8,128)(2,1)}, bf16[2048,256]{1,0:T(8,128)(2,1)}) custom-call(s32[16]{0:T(128)} %get-tuple-element.134.first_ref, s32[16]{0:T(128)} %get-tuple-element.133.last_ref, bf16[2048,256]{1,0:T(8,128)(2,1)} %get-tuple-element.46.q_ref, bf16[2048,256]{1,0:T(8,128)(2,1)} %get-tuple-element.47.k_ref, ...), custom_call_target="tpu_custom_call" | custom-call | flops 5000000000 | bytes 16777216 | tf_op jit(solution)/shard_map/attend_back/pallas_call | solution.py:204
  334.1 7.6 %shard_map.241 = bf16[1024,768]{1,0:T(8,128)(2,1)} custom-call(s32[1]{0:T(128)} %bitcast.index_ref, bf16[512,1024]{1,0:T(8,128)(2,1)} %copy-done.5, bf16[512,1024]{1,0:T(8,128)(2,1)} %collective-permute-done.b_ref.refs_1_, bf16[512,1024]{1,0:T(8,128)(2,1)} %copy-done.11, bf16[512,1024]{1,0:T(8,128)(2,1)} %copy-done.12, ...), custom_call_target="tpu_custom_call" | custom-call | flops 805306368 | bytes 3407872 | tf_op jit(solution)/shard_map/pallas_call | solution.py:350
  343.6 5.5 shard_map.242
  372.1 8.1 %collective-permute-start.36 = (bf16[256,512]{1,0:T(8,128)(2,1)S(1)}, bf16[256,512]{1,0:T(8,128)(2,1)S(1)}, u32[]{:S(2)}, u32[]{:S(2)}) collective-permute-start(bf16[256,512]{1,0:T(8,128)(2,1)S(1)} %constant_dynamic-slice_fusion), channel_id=1, source_target_pairs={{0,16},{4,20},{8,24},{12,28},{16,0},{20,4},{24,8},{28,12},{1,17},{... | collective-permute-start | bytes 786440 | tf_op jit(solution)/shard_map/ppermute | solution.py:222
  381.4 21.6 %collective-permute-done.36 = bf16[256,512]{1,0:T(8,128)(2,1)S(1)} collective-permute-done((bf16[256,512]{1,0:T(8,128)(2,1)S(1)}, bf16[256,512]{1,0:T(8,128)(2,1)S(1)}, u32[]{:S(2)}, u32[]{:S(2)}) %collective-permute-start.36) | collective-permute-done | bytes 262176 | tf_op jit(solution)/shard_map/ppermute | solution.py:222
  403.2 7.4 %collective-permute-done.30 = bf16[256,512]{1,0:T(8,128)(2,1)S(1)} collective-permute-done((bf16[256,512]{1,0:T(8,128)(2,1)S(1)}, bf16[256,512]{1,0:T(8,128)(2,1)S(1)}, u32[]{:S(2)}, u32[]{:S(2)}) %collective-permute-start.30) | collective-permute-done | bytes 262176 | tf_op jit(solution)/shard_map/ppermute | solution.py:222
  412.5 6.5 %collective-permute-done.37 = bf16[128,512]{1,0:T(8,128)(2,1)S(1)} collective-permute-done((bf16[128,512]{1,0:T(8,128)(2,1)S(1)}, bf16[128,512]{1,0:T(8,128)(2,1)S(1)}, u32[]{:S(2)}, u32[]{:S(2)}) %collective-permute-start.37) | collective-permute-done | bytes 131104 | tf_op jit(solution)/shard_map/ppermute | solution.py:222
  419.1 15.4 %collective-permute-done.31 = bf16[128,512]{1,0:T(8,128)(2,1)S(1)} collective-permute-done((bf16[128,512]{1,0:T(8,128)(2,1)S(1)}, bf16[128,512]{1,0:T(8,128)(2,1)S(1)}, u32[]{:S(2)}, u32[]{:S(2)}) %collective-permute-start.31) | collective-permute-done | bytes 131104 | tf_op jit(solution)/shard_map/ppermute | solution.py:222
  442.9 33.9 %collective-permute-done.39 = bf16[256,512]{1,0:T(8,128)(2,1)S(1)} collective-permute-done((bf16[256,512]{1,0:T(8,128)(2,1)S(1)}, bf16[256,512]{1,0:T(8,128)(2,1)S(1)}, u32[]{:S(2)}, u32[]{:S(2)}) %collective-permute-start.39) | collective-permute-done | bytes 262176 | tf_op jit(solution)/shard_map/ppermute | solution.py:222
  483.8 53.2 %collective-permute-done.33 = bf16[256,512]{1,0:T(8,128)(2,1)S(1)} collective-permute-done((bf16[256,512]{1,0:T(8,128)(2,1)S(1)}, bf16[256,512]{1,0:T(8,128)(2,1)S(1)}, u32[]{:S(2)}, u32[]{:S(2)}) %collective-permute-start.33) | collective-permute-done | bytes 262176 | tf_op jit(solution)/shard_map/ppermute | solution.py:222
  543.5 7.7 %collective-permute-done.34 = bf16[512,512]{1,0:T(8,128)(2,1)S(1)} collective-permute-done((bf16[512,512]{1,0:T(8,128)(2,1)S(1)}, bf16[512,512]{1,0:T(8,128)(2,1)S(1)}, u32[]{:S(2)}, u32[]{:S(2)}) %collective-permute-start.34) | collective-permute-done | bytes 524320 | tf_op jit(solution)/shard_map/ppermute | solution.py:222
  (225 shorter events, 149.9 us)
Async XLA Ops:
  7.2 560.9 %all-reduce.3.cloned.1.call-start = ((), (), s32[]{:S(2)}) async-start(), calls=%async_computation | async-start | bytes 12582912 | tf_op jit(solution)/shard_map/psum | solution.py:504
  10.9 26.2 %collective-permute-start.1 = (bf16[512,1024]{1,0:T(8,128)(2,1)S(1)}, bf16[512,1024]{1,0:T(8,128)(2,1)S(1)}, u32[]{:S(2)}, u32[]{:S(2)}) collective-permute-start(bf16[512,1024]{1,0:T(8,128)(2,1)S(1)} %fusion.7.a_ref.refs_0_), channel_id=1, source_target_pairs={{0,2},{1,3},{2,0},{3,1},{4,6},{5,7},{6,4},{7,5},{8,10},{9,11},{10,... | collective-permute-start | bytes 3145736 | tf_op jit(solution)/shard_map/ppermute | solution.py:222
  14.0 30.0 %collective-permute-start = (bf16[512,1024]{1,0:T(8,128)(2,1)S(1)}, bf16[512,1024]{1,0:T(8,128)(2,1)}, u32[]{:S(2)}, u32[]{:S(2)}) collective-permute-start(bf16[512,1024]{1,0:T(8,128)(2,1)S(1)} %fusion.7.a_ref.refs_0_), channel_id=1, source_target_pairs={{0,1},{1,0},{2,3},{3,2},{4,5},{5,4},{6,7},{7,6},{8,9},{9,8},{10,11... | collective-permute-start | bytes 3145736 | tf_op jit(solution)/shard_map/ppermute | solution.py:222
  89.0 26.1 %collective-permute-start.5 = (bf16[512,1024]{1,0:T(8,128)(2,1)S(1)}, bf16[512,1024]{1,0:T(8,128)(2,1)S(1)}, u32[]{:S(2)}, u32[]{:S(2)}) collective-permute-start(bf16[512,1024]{1,0:T(8,128)(2,1)S(1)} %add_convert_fusion.9), channel_id=1, source_target_pairs={{0,2},{1,3},{2,0},{3,1},{4,6},{5,7},{6,4},{7,5},{8,10},{9,11},{10,... | collective-permute-start | bytes 3145736 | tf_op jit(solution)/shard_map/ppermute | solution.py:222
  90.9 46.9 %collective-permute-start.11 = (bf16[512,1024]{1,0:T(8,128)(2,1)}, bf16[512,1024]{1,0:T(8,128)(2,1)}, u32[]{:S(2)}, u32[]{:S(2)}) collective-permute-start(bf16[512,1024]{1,0:T(8,128)(2,1)} %refs_4_.8), channel_id=1, source_target_pairs={{0,2},{1,3},{2,0},{3,1},{4,6},{5,7},{6,4},{7,5},{8,10},{9,11},{10,... | collective-permute-start | bytes 3145736 | tf_op jit(solution)/shard_map/ppermute | solution.py:222
  116.9 42.8 %collective-permute-start.9 = (bf16[512,1024]{1,0:T(8,128)(2,1)S(1)}, bf16[512,1024]{1,0:T(8,128)(2,1)}, u32[]{:S(2)}, u32[]{:S(2)}) collective-permute-start(bf16[512,1024]{1,0:T(8,128)(2,1)S(1)} %add_convert_fusion.8.refs_0_), channel_id=1, source_target_pairs={{0,2},{1,3},{2,0},{3,1},{4,6},{5,7},{6,4},{7,5},{8,10},{9,11},{10,... | collective-permute-start | bytes 3145736 | tf_op jit(solution)/shard_map/ppermute | solution.py:222
  118.7 41.0 %collective-permute-start.7 = (bf16[512,1024]{1,0:T(8,128)(2,1)}, bf16[512,1024]{1,0:T(8,128)(2,1)}, u32[]{:S(2)}, u32[]{:S(2)}) collective-permute-start(bf16[512,1024]{1,0:T(8,128)(2,1)} %refs_4_.8), channel_id=1, source_target_pairs={{0,1},{1,0},{2,3},{3,2},{4,5},{5,4},{6,7},{7,6},{8,9},{9,8},{10,11... | collective-permute-start | bytes 3145736 | tf_op jit(solution)/shard_map/ppermute | solution.py:222
  118.7 41.0 %collective-permute-start.6 = (bf16[512,1024]{1,0:T(8,128)(2,1)S(1)}, bf16[512,1024]{1,0:T(8,128)(2,1)}, u32[]{:S(2)}, u32[]{:S(2)}) collective-permute-start(bf16[512,1024]{1,0:T(8,128)(2,1)S(1)} %add_convert_fusion.8.refs_0_), channel_id=1, source_target_pairs={{0,1},{1,0},{2,3},{3,2},{4,5},{5,4},{6,7},{7,6},{8,9},{9,8},{10,11... | collective-permute-start | bytes 3145736 | tf_op jit(solution)/shard_map/ppermute | solution.py:222
  137.7 38.1 %collective-permute-start.12 = (bf16[512,1024]{1,0:T(8,128)(2,1)}, bf16[512,1024]{1,0:T(8,128)(2,1)}, u32[]{:S(2)}, u32[]{:S(2)}) collective-permute-start(bf16[512,1024]{1,0:T(8,128)(2,1)} %collective-permute-done.11.refs_2_.refs_6_), channel_id=1, source_target_pairs={{0,1},{1,0},{2,3},{3,2},{4,5},{5,4},{6,7},{7,6},{8,9},{9,8},{10,11... | collective-permute-start | bytes 3145736 | tf_op jit(solution)/shard_map/ppermute | solution.py:222
  197.8 25.6 %collective-permute-start.16 = (bf16[512,1024]{1,0:T(8,128)(2,1)S(1)}, bf16[512,1024]{1,0:T(8,128)(2,1)S(1)}, u32[]{:S(2)}, u32[]{:S(2)}) collective-permute-start(bf16[512,1024]{1,0:T(8,128)(2,1)S(1)} %add_convert_fusion.2), channel_id=1, source_target_pairs={{0,2},{1,3},{2,0},{3,1},{4,6},{5,7},{6,4},{7,5},{8,10},{9,11},{10,... | collective-permute-start | bytes 3145736 | tf_op jit(solution)/shard_map/ppermute | solution.py:222
  229.6 25.0 %collective-permute-start.17 = (bf16[512,1024]{1,0:T(8,128)(2,1)}, bf16[512,1024]{1,0:T(8,128)(2,1)}, u32[]{:S(2)}, u32[]{:S(2)}) collective-permute-start(bf16[512,1024]{1,0:T(8,128)(2,1)} %get-tuple-element.118.a_ref.refs_0_), channel_id=1, source_target_pairs={{0,2},{1,3},{2,0},{3,1},{4,6},{5,7},{6,4},{7,5},{8,10},{9,11},{10,... | collective-permute-start | bytes 3145736 | tf_op jit(solution)/shard_map/ppermute | solution.py:222
  235.7 242.8 %collective-permute-start.8 = (bf16[512,1024]{1,0:T(8,128)(2,1)}, bf16[512,1024]{1,0:T(8,128)(2,1)}, u32[]{:S(2)}, u32[]{:S(2)}) collective-permute-start(bf16[512,1024]{1,0:T(8,128)(2,1)} %convolution_convert_fusion.2), channel_id=1, source_target_pairs={{0,1},{1,0},{2,3},{3,2},{4,5},{5,4},{6,7},{7,6},{8,9},{9,8},{10,11... | collective-permute-start | bytes 3145736 | tf_op jit(solution)/shard_map/ppermute | solution.py:222
  235.7 51.4 %collective-permute-start.19 = (bf16[512,1024]{1,0:T(8,128)(2,1)}, bf16[512,1024]{1,0:T(8,128)(2,1)}, u32[]{:S(2)}, u32[]{:S(2)}) collective-permute-start(bf16[512,1024]{1,0:T(8,128)(2,1)} %get-tuple-element.118.a_ref.refs_0_), channel_id=1, source_target_pairs={{0,1},{1,0},{2,3},{3,2},{4,5},{5,4},{6,7},{7,6},{8,9},{9,8},{10,11... | collective-permute-start | bytes 3145736 | tf_op jit(solution)/shard_map/ppermute | solution.py:222
  254.6 32.5 %collective-permute-start.20 = (bf16[512,1024]{1,0:T(8,128)(2,1)}, bf16[512,1024]{1,0:T(8,128)(2,1)}, u32[]{:S(2)}, u32[]{:S(2)}) collective-permute-start(bf16[512,1024]{1,0:T(8,128)(2,1)} %collective-permute-done.17.c_ref.refs_2_), channel_id=1, source_target_pairs={{0,1},{1,0},{2,3},{3,2},{4,5},{5,4},{6,7},{7,6},{8,9},{9,8},{10,11... | collective-permute-start | bytes 3145736 | tf_op jit(solution)/shard_map/ppermute | solution.py:222
  259.6 92.1 %collective-permute-start.13 = (bf16[512,1024]{1,0:T(8,128)(2,1)}, bf16[512,1024]{1,0:T(8,128)(2,1)}, u32[]{:S(2)}, u32[]{:S(2)}) collective-permute-start(bf16[512,1024]{1,0:T(8,128)(2,1)} %convolution_convert_fusion), channel_id=1, source_target_pairs={{0,1},{1,0},{2,3},{3,2},{4,5},{5,4},{6,7},{7,6},{8,9},{9,8},{10,11... | collective-permute-start | bytes 3145736 | tf_op jit(solution)/shard_map/ppermute | solution.py:222
  354.5 126.0 %collective-permute-start.18 = (bf16[512,1024]{1,0:T(8,128)(2,1)}, bf16[512,1024]{1,0:T(8,128)(2,1)}, u32[]{:S(2)}, u32[]{:S(2)}) collective-permute-start(bf16[512,1024]{1,0:T(8,128)(2,1)} %add_convert_fusion.7), channel_id=1, source_target_pairs={{0,2},{1,3},{2,0},{3,1},{4,6},{5,7},{6,4},{7,5},{8,10},{9,11},{10,... | collective-permute-start | bytes 3145736 | tf_op jit(solution)/shard_map/ppermute | solution.py:222
  363.4 177.1 %collective-permute-start.21 = (bf16[512,1024]{1,0:T(8,128)(2,1)}, bf16[512,1024]{1,0:T(8,128)(2,1)}, u32[]{:S(2)}, u32[]{:S(2)}) collective-permute-start(bf16[512,1024]{1,0:T(8,128)(2,1)} %get-tuple-element.74), channel_id=1, source_target_pairs={{0,1},{1,0},{2,3},{3,2},{4,5},{5,4},{6,7},{7,6},{8,9},{9,8},{10,11... | collective-permute-start | bytes 3145736 | tf_op jit(solution)/shard_map/ppermute | solution.py:222
  370.8 68.7 %collective-permute-start.22 = (bf16[512,1024]{1,0:T(8,128)(2,1)}, bf16[512,1024]{1,0:T(8,128)(2,1)S(1)}, u32[]{:S(2)}, u32[]{:S(2)}) collective-permute-start(bf16[512,1024]{1,0:T(8,128)(2,1)} %get-tuple-element.76), channel_id=1, source_target_pairs={{0,1},{1,0},{2,3},{3,2},{4,5},{5,4},{6,7},{7,6},{8,9},{9,8},{10,11... | collective-permute-start | bytes 3145736 | tf_op jit(solution)/shard_map/ppermute | solution.py:222
  372.1 30.9 %collective-permute-start.36 = (bf16[256,512]{1,0:T(8,128)(2,1)S(1)}, bf16[256,512]{1,0:T(8,128)(2,1)S(1)}, u32[]{:S(2)}, u32[]{:S(2)}) collective-permute-start(bf16[256,512]{1,0:T(8,128)(2,1)S(1)} %constant_dynamic-slice_fusion), channel_id=1, source_target_pairs={{0,16},{4,20},{8,24},{12,28},{16,0},{20,4},{24,8},{28,12},{1,17},{... | collective-permute-start | bytes 786440 | tf_op jit(solution)/shard_map/ppermute | solution.py:222
  439.4 38.9 %collective-permute-start.32 = (bf16[128,512]{1,0:T(8,128)(2,1)S(1)}, bf16[128,512]{1,0:T(8,128)(2,1)S(1)}, u32[]{:S(2)}, u32[]{:S(2)}) collective-permute-start(bf16[128,512]{1,0:T(8,128)(2,1)S(1)} %add_convert_fusion.15), channel_id=1, source_target_pairs={{0,16},{4,20},{8,24},{12,28},{16,0},{20,4},{24,8},{28,12},{1,17},{... | collective-permute-start | bytes 393224 | tf_op jit(solution)/shard_map/ppermute | solution.py:222
  439.5 37.3 %collective-permute-start.39 = (bf16[256,512]{1,0:T(8,128)(2,1)S(1)}, bf16[256,512]{1,0:T(8,128)(2,1)S(1)}, u32[]{:S(2)}, u32[]{:S(2)}) collective-permute-start(bf16[256,512]{1,0:T(8,128)(2,1)S(1)} %maximum_select_fusion.5), channel_id=1, source_target_pairs={{0,16},{4,20},{8,24},{12,28},{16,0},{20,4},{24,8},{28,12},{1,17},{... | collective-permute-start | bytes 786440 | tf_op jit(solution)/shard_map/ppermute | solution.py:222
  476.8 63.8 %collective-permute-start.23 = (bf16[512,1024]{1,0:T(8,128)(2,1)S(1)}, bf16[512,1024]{1,0:T(8,128)(2,1)S(1)}, u32[]{:S(2)}, u32[]{:S(2)}) collective-permute-start(bf16[512,1024]{1,0:T(8,128)(2,1)S(1)} %add_convert_fusion), channel_id=1, source_target_pairs={{0,2},{1,3},{2,0},{3,1},{4,6},{5,7},{6,4},{7,5},{8,10},{9,11},{10,... | collective-permute-start | bytes 3145736 | tf_op jit(solution)/shard_map/ppermute | solution.py:222
  478.3 60.2 %collective-permute-start.40 = (bf16[512,512]{1,0:T(8,128)(2,1)S(1)}, bf16[512,512]{1,0:T(8,128)(2,1)S(1)}, u32[]{:S(2)}, u32[]{:S(2)}) collective-permute-start(bf16[512,512]{1,0:T(8,128)(2,1)S(1)} %maximum_select_fusion.3), channel_id=1, source_target_pairs={{0,8},{4,12},{8,0},{12,4},{16,24},{20,28},{24,16},{28,20},{1,9},{5... | collective-permute-start | bytes 1572872 | tf_op jit(solution)/shard_map/ppermute | solution.py:222
  478.5 58.5 %collective-permute-start.33 = (bf16[256,512]{1,0:T(8,128)(2,1)S(1)}, bf16[256,512]{1,0:T(8,128)(2,1)S(1)}, u32[]{:S(2)}, u32[]{:S(2)}) collective-permute-start(bf16[256,512]{1,0:T(8,128)(2,1)S(1)} %maximum_select_fusion.4), channel_id=1, source_target_pairs={{0,8},{4,12},{8,0},{12,4},{16,24},{20,28},{24,16},{28,20},{1,9},{5... | collective-permute-start | bytes 786440 | tf_op jit(solution)/shard_map/ppermute | solution.py:222
  (52 other events, 479.1 us)
Sparse Core Ops, SparseCore 0:
  283.1 254.3 all-reduce.2
